TPU v7x, 256 devices: a 8x8x2 block of a 8x8x16 slice. The times are simulated.
256 devices in a mesh: groups: 2 (over z), ep: 64 (over y, x), tp: 2 (over core).
Axes of the slice: x: 8, y: 8, z: 2, core: 2. Of those that a mesh axis runs over, the one named last changes fastest.
The devices are a block of a 8x8x16 slice.
Arguments:
- hidden: bfloat16 [2048, 3584], P(('groups', 'ep'), 'tp'), parts along dimension 0, may hold values from -6 to 6
- routes: int32 [2048, 8], P(('groups', 'ep')), parts along dimension 0, may hold values from 0 to 63, as said below
- router_weight: bfloat16 [3584, 64], P('tp'), may hold values from -0.1875 to 0.1875
- gate_weight: bfloat16 [64, 3584, 1024], P('ep', None, 'tp'), may hold values from -0.09375 to 0.09375
- up_weight: bfloat16 [64, 3584, 1024], P('ep', None, 'tp'), may hold values from -0.09375 to 0.09375
- down_weight: bfloat16 [64, 1024, 3584], P('ep', 'tp'), may hold values from -0.1875 to 0.1875
- q_latent: bfloat16 [512, 64, 512], P(('groups', 'ep'), 'tp'), parts along dimension 0, may hold values from -48 to 48
- q_rope: bfloat16 [512, 64, 64], P(('groups', 'ep'), 'tp'), parts along dimension 0, may hold values from -48 to 48
- cache_latent: bfloat16 [512, 256, 512], P(('groups', 'ep')), parts along dimension 0, may hold values from -4 to 4
- cache_rope: bfloat16 [512, 64, 256], P(('groups', 'ep')), parts along dimension 0, may hold values from -4 to 4
- lengths: int32 [512], P(('groups', 'ep')), parts along dimension 0, may hold values from 16 to 256, as said below
Outputs:
- moe_out: bfloat16 [2048, 3584], P(('groups', 'ep'), 'tp'), parts along dimension 0
- attn_latent: bfloat16 [512, 64, 512], P(('groups', 'ep'), 'tp'), parts along dimension 0
There are 2 independent parts, one for each index of `groups`. A program takes and returns all parts, laid end to end along the dimension named above; an argument that names none is the same for every part. Nothing has to cross between parts.
Inputs may be any that keep to these rules, and one draw needn't show every extreme that they name: `routes`: each row names 8 different experts; in each aligned block of 16 rows (the rows of one index of ep) no expert is named more than 8 times, and one expert, the same in every block, is named exactly 8 times in each block. `lengths`: one sequence has 256 live positions and one has 16.
All inputs are finite; a program needn't handle non-finite values.
Results may differ from a plain program's by a relative error of at most 0.0085.
Values may be sent and summed in bfloat16 or wider, within the bound.
No kernel may reach another device: no remote copies, remote signals or barrier semaphores. Data moves between devices by JAX's collectives and lax.ppermute only.
A program may use at most 128 MiB of HBM per device.

v0:
```python
import jax
import jax.numpy as jnp
from jax import lax
from jax.sharding import PartitionSpec as P

softmax_scale = 192.0 ** (-0.5)
routed_scale = 2.5


def gathered_total(value, axis):
    tiles = lax.all_gather(value, axis)
    return tiles.sum(axis=0)


def in_blocks(value, dim, devices):
    lengths = value.shape
    tiles = value.reshape(*lengths[:dim], devices, lengths[dim] // devices, *lengths[dim + 1 :])
    return jnp.moveaxis(tiles, dim, 0)


def sum_at_owner(value, axis, dim):
    devices = lax.axis_size(axis)
    tiles = lax.all_to_all(in_blocks(value, dim, devices), axis, 0, 0, tiled=True)
    return jnp.sum(tiles, axis=0)


def local(
    hidden,
    routes,
    router_weight,
    gate_weight,
    up_weight,
    down_weight,
    q_latent,
    q_rope,
    cache_latent,
    cache_rope,
    lengths,
):
    token_count, top_count = routes.shape
    expert_count = lax.axis_size("ep")
    capacity = min(token_count, 4 * token_count * top_count // expert_count)
    partial_logits = jnp.dot(hidden, router_weight, preferred_element_type=jnp.float32)
    logits = gathered_total(partial_logits, "tp")
    affinity = jax.nn.sigmoid(logits)
    expert_iota = jnp.arange(expert_count, dtype=jnp.int32)
    chosen_mask = routes[:, :, None] == expert_iota[None, None, :]
    chosen = jnp.sum(jnp.where(chosen_mask, affinity[:, None, :], 0.0), axis=2)
    gates = routed_scale * chosen / jnp.sum(chosen, axis=1, keepdims=True)
    flat_mask = chosen_mask.reshape(token_count * top_count, expert_count).astype(jnp.int32)
    earlier = jnp.cumsum(flat_mask, axis=0) - flat_mask
    within = jnp.sum(flat_mask * earlier, axis=1).reshape(token_count, top_count)
    slot_index = routes * capacity + within
    slot_iota = jnp.arange(expert_count * capacity, dtype=jnp.int32)
    placing = jnp.sum(
        (slot_index[None, :, :] == slot_iota[:, None, None]).astype(jnp.int32), axis=2
    )
    placing = placing.astype(jnp.bfloat16)
    outgoing = jnp.dot(placing, hidden, preferred_element_type=jnp.float32).astype(jnp.bfloat16)
    outgoing = outgoing.reshape(expert_count, capacity, hidden.shape[1])
    received = lax.all_to_all(outgoing, "ep", split_axis=0, concat_axis=0, tiled=True)
    received = lax.all_gather(received, "tp", axis=2, tiled=True)
    source_count, slot_count, feature_count = received.shape
    flat_rows = received.reshape(source_count * slot_count, feature_count)
    gate_part = jnp.dot(flat_rows, gate_weight[0], preferred_element_type=jnp.float32)
    up_part = jnp.dot(flat_rows, up_weight[0], preferred_element_type=jnp.float32)
    active = (jax.nn.silu(gate_part) * up_part).astype(jnp.bfloat16)
    partial_out = jnp.dot(active, down_weight[0], preferred_element_type=jnp.float32)
    summed = sum_at_owner(partial_out, "tp", 1).astype(jnp.bfloat16)
    summed = summed.reshape(source_count, slot_count, summed.shape[1])
    returned = lax.all_to_all(summed, "ep", split_axis=0, concat_axis=0, tiled=True)
    scores = jnp.einsum("bhl,bjl->bhj", q_latent, cache_latent, preferred_element_type=jnp.float32)
    scores = scores + jnp.einsum(
        "bhr,brj->bhj", q_rope, cache_rope, preferred_element_type=jnp.float32
    )
    scores = scores * softmax_scale
    position = jnp.arange(cache_latent.shape[1], dtype=jnp.int32)
    live = position[None, None, :] < lengths[:, None, None]
    scores = jnp.where(live, scores, -jnp.inf)
    highest = jnp.max(scores, axis=2, keepdims=True)
    expo = jnp.where(live, jnp.exp(scores - highest), 0.0)
    attn_probs = (expo / jnp.sum(expo, axis=2, keepdims=True)).astype(jnp.bfloat16)
    attn_latent = jnp.einsum(
        "bhj,bjl->bhl", attn_probs, cache_latent, preferred_element_type=jnp.float32
    )
    attn_latent = attn_latent.astype(jnp.bfloat16)
    returned_flat = returned.reshape(expert_count * capacity, returned.shape[2])
    picked = jnp.take(returned_flat, slot_index.reshape(-1), axis=0).reshape(
        token_count, top_count, returned.shape[2]
    )
    moe_out = jnp.sum(gates[:, :, None] * picked.astype(jnp.float32), axis=1).astype(jnp.bfloat16)
    return (moe_out, attn_latent)


def solution(mesh):
    return jax.shard_map(
        local,
        mesh=mesh,
        in_specs=(
            P(("groups", "ep"), "tp"),
            P(("groups", "ep"), None),
            P("tp", None),
            P("ep", None, "tp"),
            P("ep", None, "tp"),
            P("ep", "tp", None),
            P(("groups", "ep"), "tp", None),
            P(("groups", "ep"), "tp", None),
            P(("groups", "ep"), None, None),
            P(("groups", "ep"), None, None),
            P(("groups", "ep")),
        ),
        out_specs=(P(("groups", "ep"), "tp"), P(("groups", "ep"), "tp", None)),
        check_vma=False,
    )
```

profile of v0, /device:TPU:514, one launch (start us, length us, event | category | flops | bytes accessed | tf_op | source)
XLA Modules:
  0.0 199.2 jit_solution(17828745028653575509)
XLA Ops:
  7.3 0.8 copy.21
  8.3 0.2 reduce_window_sum.11
  8.5 0.2 select_reduce_fusion.2
  8.7 0.1 convert_reduce_fusion
  8.9 1.5 fusion.7
  10.4 66.5 %all_to_all.15 = bf16[64,8,1792]{2,1,0:T(8,128)(2,1)} all-to-all(bf16[64,8,1792]{2,1,0:T(8,128)(2,1)S(1)} %fusion.7), channel_id=1, replica_groups=mesh['groups'=2,'ep'=64,'tp'=2] {'ep'}, dimensions={0} | all-to-all | bytes 3670016 | tf_op jit(solution)/shard_map/all_to_all | solution.py:61
  77.0 6.0 %copy.25 = bf16[3584,512]{1,0:T(8,128)(2,1)} copy(bf16[3584,512]{0,1:T(8,128)(2,1)} %bitcast.59) | data formatting | bytes 7340032 | tf_op jit(solution)/shard_map/dot_general | solution.py:68
  82.9 20.7 %all-gather.3.cloned.1.call-done = bf16[64,8,3584]{2,1,0:T(8,128)(2,1)} async-done(((bf16[64,8,1792]{2,1,0:T(8,128)(2,1)}), bf16[64,8,3584]{2,1,0:T(8,128)(2,1)}) %all-gather.3.cloned.1.call-update) | async-done | bytes 3670032 | tf_op jit(solution)/shard_map/all_gather | solution.py:62
  103.6 5.3 %fusion.3 = f32[512,512]{1,0:T(8,128)S(1)} fusion(bf16[1,3584,512]{2,1,0:T(8,128)(2,1)} %param.14, bf16[64,8,3584]{2,1,0:T(8,128)(2,1)} %all-gather.3.cloned.1.call-done), kind=kOutput, calls=%fused_computation.5 | convolution fusion | flops 1879048192 | bytes 8388608 | tf_op jit(solution)/shard_map/dot_general | solution.py:65
  109.0 2.1 %fusion.18 = bf16[512,512,1]{1,0,2:T(8,128)(2,1)S(1)} fusion(bf16[1,3584,512]{2,1,0:T(8,128)(2,1)S(1)} %copy-done.7, bf16[64,8,3584]{2,1,0:T(8,128)(2,1)S(1)} %copy-done.8, f32[512,512]{1,0:T(8,128)S(1)} %fusion.3), kind=kOutput, calls=%fused_computation.14 | convolution fusion | flops 1880621056 | bytes 8912896 | tf_op jit(solution)/shard_map/dot_general | solution.py:66
  111.2 2.1 %convolution_bitcast_fusion = f32[2,512,1792]{2,1,0:T(8,128)S(1)} fusion(bf16[512,512,1]{1,0,2:T(8,128)(2,1)S(1)} %fusion.18, bf16[2,1792,512]{2,1,0:T(8,128)(2,1)S(1)} %bitcast.57), kind=kOutput, calls=%fused_computation.2 | convolution fusion | flops 1879048192 | bytes 11534336 | tf_op jit(solution)/shard_map/dot_general | solution.py:68
  113.3 10.9 %all_to_all.16 = f32[2,512,1792]{2,1,0:T(8,128)} all-to-all(f32[2,512,1792]{2,1,0:T(8,128)S(1)} %convolution_bitcast_fusion), channel_id=1, replica_groups=mesh['groups'=2,'ep'=64,'tp'=2] {'tp'}, dimensions={0} | all-to-all | bytes 14680064 | tf_op jit(solution)/shard_map/all_to_all | solution.py:23
  124.2 5.5 %reduce_sum.77 = bf16[512,1792]{1,0:T(8,128)(2,1)} reduce(f32[2,512,1792]{2,1,0:T(8,128)} %all_to_all.16, f32[]{:T(128)} %constant.13.clone.1), dimensions={0}, to_apply=%region_6.7 | reduce | flops 917504 | bytes 9175044 | tf_op jit(solution)/shard_map/reduce_sum | solution.py:24
  129.7 13.8 %all-to-all-start.2 = ((bf16[64,8,1792]{2,1,0:T(8,128)(2,1)}), bf16[64,8,1792]{2,1,0:T(8,128)(2,1)S(1)}, u32[]{:S(2)}, u32[]{:S(2)}) async-start(bf16[64,8,1792]{2,1,0:T(8,128)(2,1)} %bitcast.58), calls=%async_computation.2 | async-start | bytes 3670016 | tf_op jit(solution)/shard_map/all_to_all | solution.py:71
  143.6 0.1 fusion.35
  143.8 1.9 all-gather
  145.7 0.3 select_reduce_fusion
  146.1 0.4 fusion.36
  146.5 0.1 fusion.27
  146.7 0.2 fusion.34
  146.9 1.0 convolution_convert_fusion.1
  147.9 42.2 %all-to-all-done.2 = bf16[64,8,1792]{2,1,0:T(8,128)(2,1)S(1)} async-done(((bf16[64,8,1792]{2,1,0:T(8,128)(2,1)}), bf16[64,8,1792]{2,1,0:T(8,128)(2,1)S(1)}, u32[]{:S(2)}, u32[]{:S(2)}) %all-to-all-start.2) | async-done | bytes 1835040 | tf_op jit(solution)/shard_map/all_to_all | solution.py:71
  190.1 0.9 gather_fusion
  191.0 1.3 multiply_reduce_fusion
  (33 shorter events, 0.7 us)
Async XLA Ops:
  7.2 138.9 %copy-start = (bf16[4,256,512]{2,1,0:T(8,128)(2,1)S(1)}, bf16[4,256,512]{2,1,0:T(8,128)(2,1)}, u32[]{:S(2)}) copy-start(bf16[4,256,512]{2,1,0:T(8,128)(2,1)} %param.19) | copy-start | bytes 3145732
  7.2 96.4 %all-gather.3.cloned.1.call-start = ((), (), s32[]{:S(2)}) async-start(), calls=%async_computation.3 | async-start | bytes 5505024 | tf_op jit(solution)/shard_map/all_gather | solution.py:62
  103.6 5.4 %copy-start.7 = (bf16[1,3584,512]{2,1,0:T(8,128)(2,1)S(1)}, bf16[1,3584,512]{2,1,0:T(8,128)(2,1)}, u32[]{:S(2)}) copy-start(bf16[1,3584,512]{2,1,0:T(8,128)(2,1)} %param.15) | copy-start | bytes 11010052
  103.6 5.4 %copy-start.8 = (bf16[64,8,3584]{2,1,0:T(8,128)(2,1)S(1)}, bf16[64,8,3584]{2,1,0:T(8,128)(2,1)}, u32[]{:S(2)}) copy-start(bf16[64,8,3584]{2,1,0:T(8,128)(2,1)} %all-gather.3.cloned.1.call-done) | copy-start | bytes 11010052
  109.0 2.2 %copy-start.1 = (bf16[3584,512]{1,0:T(8,128)(2,1)S(1)}, bf16[3584,512]{1,0:T(8,128)(2,1)}, u32[]{:S(2)}) copy-start(bf16[3584,512]{1,0:T(8,128)(2,1)} %copy.25) | copy-start | bytes 11010052
  129.6 14.0 %copy-start.2 = (bf16[1792,64]{0,1:T(8,128)(2,1)S(1)}, bf16[1792,64]{0,1:T(8,128)(2,1)}, u32[]{:S(2)}) copy-start(bf16[1792,64]{0,1:T(8,128)(2,1)} %param.13) | copy-start | bytes 688132
  129.6 14.0 %copy-start.3 = (bf16[16,1792]{1,0:T(8,128)(2,1)S(1)}, bf16[16,1792]{1,0:T(8,128)(2,1)}, u32[]{:S(2)}) copy-start(bf16[16,1792]{1,0:T(8,128)(2,1)} %param.11) | copy-start | bytes 172036
  129.6 16.4 %copy-start.9 = (s32[4]{0:T(128)S(1)}, s32[4]{0:T(128)}, u32[]{:S(2)}) copy-start(s32[4]{0:T(128)} %param.21) | copy-start | bytes 52
  129.6 16.4 %copy-start.4 = (bf16[4,32,512]{2,1,0:T(8,128)(2,1)S(1)}, bf16[4,32,512]{2,1,0:T(8,128)(2,1)}, u32[]{:S(2)}) copy-start(bf16[4,32,512]{2,1,0:T(8,128)(2,1)} %param.17) | copy-start | bytes 393220
  129.6 16.8 %copy-start.5 = (bf16[4,64,256]{2,1,0:T(8,128)(2,1)S(1)}, bf16[4,64,256]{2,1,0:T(8,128)(2,1)}, u32[]{:S(2)}) copy-start(bf16[4,64,256]{2,1,0:T(8,128)(2,1)} %param.20) | copy-start | bytes 393220
  129.6 16.9 %copy-start.6 = (bf16[4,32,64]{2,1,0:T(8,128)(2,1)S(1)}, bf16[4,32,64]{2,1,0:T(8,128)(2,1)}, u32[]{:S(2)}) copy-start(bf16[4,32,64]{2,1,0:T(8,128)(2,1)} %param.18) | copy-start | bytes 49156
  129.7 60.4 %all-to-all-start.2 = ((bf16[64,8,1792]{2,1,0:T(8,128)(2,1)}), bf16[64,8,1792]{2,1,0:T(8,128)(2,1)S(1)}, u32[]{:S(2)}, u32[]{:S(2)}) async-start(bf16[64,8,1792]{2,1,0:T(8,128)(2,1)} %bitcast.58), calls=%async_computation.2 | async-start | bytes 3670016 | tf_op jit(solution)/shard_map/all_to_all | solution.py:71
Sparse Core Ops, SparseCore 0:
  77.1 26.4 all-gather.2
where the time goes:
time: 200 us; the launch traced here: 199 us
  blocking collectives  79.3 us (40%)
  waiting for transfers between devices  62.9 us (31%)
  between operations  14.2 us (7%)
  starting transfers between devices  13.9 us (7%)
  matrix products  12.8 us (6%)
  local copies, waits for them, and re-layouts  8.03 us (4%)
  other arithmetic  8.02 us (4%)
    all_to_all x1, blocking collectives, local(): lax.all_to_all(outgoing, 'ep', split_axis=0, concat_axis=0, tiled=True)  66.5 us
    all_to_all x1, waiting for transfers between devices, local(): lax.all_to_all(summed, 'ep', split_axis=0, concat_axis=0, tiled=True)  42.2 us
    all_gather x1, waiting for transfers between devices, local(): received = lax.all_gather(received, 'tp', axis=2, tiled=True)  20.7 us
    all_to_all x1, starting transfers between devices, local(): lax.all_to_all(summed, 'ep', split_axis=0, concat_axis=0, tiled=True)  13.8 us
    all_to_all x1, blocking collectives, sum_at_owner(): lax.all_to_all(in_blocks(value, dim, devices), axis, 0, 0, tiled=True)  10.9 us
    dot_general x1, local copies, waits for them, and re-layouts, local(): jnp.dot(active, down_weight[0], preferred_element_type=jnp.float32)  5.96 us
    reduce_sum x1, other arithmetic, sum_at_owner(): return jnp.sum(tiles, axis=0)  5.46 us
    dot_general x1, matrix products, local(): jnp.dot(flat_rows, gate_weight[0], preferred_element_type=jnp.float32)  5.34 us
  transfers between devices with their start and end apart: 2, of which 2 were waited for; matrix products, arithmetic and copies ran while one was open for 4% of the time, Pallas kernels for 0%

commit v1 on v0

--- a/solution.py
+++ b/solution.py
@@ -59,7 +59,9 @@
     outgoing = jnp.dot(placing, hidden, preferred_element_type=jnp.float32).astype(jnp.bfloat16)
     outgoing = outgoing.reshape(expert_count, capacity, hidden.shape[1])
     received = lax.all_to_all(outgoing, "ep", split_axis=0, concat_axis=0, tiled=True)
-    received = lax.all_gather(received, "tp", axis=2, tiled=True)
+    received = jnp.concatenate(
+        lax.all_to_all(jnp.stack([received] * lax.axis_size("tp")), "tp", 0, 0), axis=2
+    )
     source_count, slot_count, feature_count = received.shape
     flat_rows = received.reshape(source_count * slot_count, feature_count)
     gate_part = jnp.dot(flat_rows, gate_weight[0], preferred_element_type=jnp.float32)

time: 200 us -> 182 us (0.910)
  blocking collectives: 79.3 us -> 25.5 us
  starting transfers between devices: 13.9 us -> 33.7 us
  waiting for transfers between devices: 62.9 us -> 78.5 us
  between operations: 14.2 us -> 0.81 us
  local copies, waits for them, and re-layouts: 8.03 us -> 15 us
  matrix products: 12.8 us -> 19 us
    all_to_all x1, blocking collectives: 66.5 us -> 6.7 us  [local(): lax.all_to_all(jnp.stack([received] * lax.axis_size('tp')), 'tp', 0, 0)]
    all_to_all x0 -> x1, waiting for transfers between devices: none -> 36.4 us  [local(): lax.all_to_all(outgoing, 'ep', split_axis=0, concat_axis=0, tiled=True)]
    all_to_all x0 -> x1, starting transfers between devices: none -> 24.3 us  [local(): lax.all_to_all(outgoing, 'ep', split_axis=0, concat_axis=0, tiled=True)]
    all_gather x1 -> x0, waiting for transfers between devices: 20.7 us -> none  [local(): received = lax.all_gather(received, 'tp', axis=2, tiled=True)]
    dot_general x1, matrix products: 2.1 us -> 11.5 us  [local(): jnp.dot(active, down_weight[0], preferred_element_type=jnp.float32)]
    all_to_all x1, blocking collectives: 10.9 us -> 17 us  [sum_at_owner(): lax.all_to_all(in_blocks(value, dim, devices), axis, 0, 0, tiled=True)]
    all_to_all x1, starting transfers between devices: 13.8 us -> 9.46 us  [local(): lax.all_to_all(summed, 'ep', split_axis=0, concat_axis=0, tiled=True)]
    reshape x0 -> x1, local copies, waits for them, and re-layouts: none -> 3.77 us  [local(): jnp.concatenate(lax.all_to_all(jnp.stack([received] * lax.axis_size('tp')...]
  transfers between devices with their start and end apart: 2 -> 2, of which waited for: 2 -> 2; matrix products, arithmetic and copies ran while one was open for 4% -> 5% of each run, Pallas kernels for 0% -> 0%
where the time goes in v1:
time: 182 us; the launch traced here: 181 us
  waiting for transfers between devices  78.5 us (43%)
  starting transfers between devices  33.7 us (19%)
  blocking collectives  25.5 us (14%)
  matrix products  19 us (10%)
  local copies, waits for them, and re-layouts  15 us (8%)
  other arithmetic  8.26 us (5%)
    all_to_all x1, waiting for transfers between devices, local(): lax.all_to_all(summed, 'ep', split_axis=0, concat_axis=0, tiled=True)  42.1 us
    all_to_all x1, waiting for transfers between devices, local(): lax.all_to_all(outgoing, 'ep', split_axis=0, concat_axis=0, tiled=True)  36.4 us
    all_to_all x1, starting transfers between devices, local(): lax.all_to_all(outgoing, 'ep', split_axis=0, concat_axis=0, tiled=True)  24.3 us
    all_to_all x1, blocking collectives, sum_at_owner(): lax.all_to_all(in_blocks(value, dim, devices), axis, 0, 0, tiled=True)  17 us
    dot_general x1, matrix products, local(): jnp.dot(active, down_weight[0], preferred_element_type=jnp.float32)  11.5 us
    all_to_all x1, starting transfers between devices, local(): lax.all_to_all(summed, 'ep', split_axis=0, concat_axis=0, tiled=True)  9.46 us
    all_to_all x1, blocking collectives, local(): lax.all_to_all(jnp.stack([received] * lax.axis_size('tp')), 'tp', 0, 0)  6.7 us
    dot_general x1, local copies, waits for them, and re-layouts, local(): jnp.dot(active, down_weight[0], preferred_element_type=jnp.float32)  5.96 us
  transfers between devices with their start and end apart: 2, of which 2 were waited for; matrix products, arithmetic and copies ran while one was open for 5% of the time, Pallas kernels for 0%

profile of v1, /device:TPU:514, one launch (start us, length us, event | category | flops | bytes accessed | tf_op | source)
XLA Modules:
  0.0 180.9 jit_solution(3517207884113823425)
XLA Ops:
  0.6 0.8 copy.26
  1.7 0.2 reduce_window_sum.11
  2.3 2.7 %fusion.5 = bf16[64,8,1792]{2,1,0:T(8,128)(2,1)} fusion(bf16[16,1792]{1,0:T(8,128)(2,1)} %param.11, s32[512,16]{0,1:T(8,128)S(1)} %convert_reduce_fusion), kind=kOutput, calls=%fused_computation.10 | convolution fusion | flops 30285824 | bytes 1925120 | tf_op jit(solution)/shard_map/dot_general | solution.py:59
  5.0 24.3 %all-to-all-start = ((bf16[64,8,1792]{2,1,0:T(8,128)(2,1)}), bf16[64,8,1792]{2,1,0:T(8,128)(2,1)S(1)}, u32[]{:S(2)}, u32[]{:S(2)}) async-start(bf16[64,8,1792]{2,1,0:T(8,128)(2,1)} %fusion.5), calls=%async_computation | async-start | bytes 3670016 | tf_op jit(solution)/shard_map/all_to_all | solution.py:61
  29.3 6.0 %copy.31 = bf16[3584,512]{1,0:T(8,128)(2,1)} copy(bf16[3584,512]{0,1:T(8,128)(2,1)} %bitcast.61) | data formatting | bytes 7340032 | tf_op jit(solution)/shard_map/dot_general | solution.py:70
  35.3 36.4 %all-to-all-done = bf16[64,8,1792]{2,1,0:T(8,128)(2,1)S(1)} async-done(((bf16[64,8,1792]{2,1,0:T(8,128)(2,1)}), bf16[64,8,1792]{2,1,0:T(8,128)(2,1)S(1)}, u32[]{:S(2)}, u32[]{:S(2)}) %all-to-all-start) | async-done | bytes 1835040 | tf_op jit(solution)/shard_map/all_to_all | solution.py:61
  71.7 0.3 pad_maximum_fusion
  72.0 6.7 %all_to_all.20 = bf16[2,64,8,1792]{3,2,1,0:T(8,128)(2,1)S(1)} all-to-all(bf16[2,64,8,1792]{3,2,1,0:T(8,128)(2,1)S(1)} %pad_maximum_fusion), channel_id=1, replica_groups=mesh['groups'=2,'ep'=64,'tp'=2] {'tp'}, dimensions={0} | all-to-all | bytes 7340032 | tf_op jit(solution)/shard_map/all_to_all | solution.py:63
  78.7 3.8 %copy.34 = bf16[64,8,2,1792]{3,2,1,0:T(2,128)(2,1)S(1)} copy(bf16[64,8,2,1792]{3,1,0,2:T(8,128)(2,1)S(1)} %bitcast.58) | data formatting | bytes 7340032 | tf_op jit(solution)/shard_map/reshape | solution.py:62
  82.5 0.6 copy.32
  83.1 2.6 %copy-done.7 = bf16[1,3584,512]{2,1,0:T(8,128)(2,1)S(1)} copy-done((bf16[1,3584,512]{2,1,0:T(8,128)(2,1)S(1)}, bf16[1,3584,512]{2,1,0:T(8,128)(2,1)}, u32[]{:S(2)}) %copy-start.7) | copy-done | bytes 3670040
  85.8 3.1 %fusion.3 = f32[512,512]{1,0:T(8,128)} fusion(bf16[512,3584]{1,0:T(8,128)(2,1)S(1)} %bitcast.63, bf16[1,3584,512]{2,1,0:T(8,128)(2,1)S(1)} %copy-done.7), kind=kOutput, calls=%fused_computation.6 | convolution fusion | flops 1879048192 | bytes 8388608 | tf_op jit(solution)/shard_map/dot_general | solution.py:67
  88.8 11.5 %convolution_bitcast_fusion = f32[2,512,1792]{2,1,0:T(8,128)} fusion(bf16[2,1792,512]{2,1,0:T(8,128)(2,1)} %bitcast.62, bf16[512,3584]{1,0:T(8,128)(2,1)} %bitcast.64, bf16[1,3584,512]{2,1,0:T(8,128)(2,1)} %param.15, f32[512,512]{1,0:T(8,128)} %fusion.3), kind=kOutput, calls=%fused_computation.2 | convolution fusion | flops 3759669248 | bytes 19398656 | tf_op jit(solution)/shard_map/dot_general | solution.py:70
  100.3 17.0 %all_to_all.21 = f32[2,512,1792]{2,1,0:T(8,128)} all-to-all(f32[2,512,1792]{2,1,0:T(8,128)} %convolution_bitcast_fusion), channel_id=1, replica_groups=mesh['groups'=2,'ep'=64,'tp'=2] {'tp'}, dimensions={0} | all-to-all | bytes 14680064 | tf_op jit(solution)/shard_map/all_to_all | solution.py:23
  117.3 5.4 %reduce_sum.77 = bf16[512,1792]{1,0:T(8,128)(2,1)} reduce(f32[2,512,1792]{2,1,0:T(8,128)} %all_to_all.21, f32[]{:T(128)} %constant.13.clone.1), dimensions={0}, to_apply=%region_6.7 | reduce | flops 917504 | bytes 9175044 | tf_op jit(solution)/shard_map/reduce_sum | solution.py:24
  122.7 9.5 %all-to-all-start.3 = ((bf16[64,8,1792]{2,1,0:T(8,128)(2,1)}), bf16[64,8,1792]{2,1,0:T(8,128)(2,1)S(1)}, u32[]{:S(2)}, u32[]{:S(2)}) async-start(bf16[64,8,1792]{2,1,0:T(8,128)(2,1)} %bitcast.59), calls=%async_computation.3 | async-start | bytes 3670016 | tf_op jit(solution)/shard_map/all_to_all | solution.py:73
  132.4 1.9 %all-gather = f32[32,64]{1,0:T(8,128)S(1)} all-gather(f32[16,64]{1,0:T(8,128)S(1)} %fusion.31), channel_id=2, replica_groups=mesh['groups'=2,'ep'=64,'tp'=2] {'tp'}, dimensions={0}, use_global_device_ids=true | all-gather | bytes 12288 | tf_op jit(solution)/shard_map/all_gather | solution.py:11
  134.3 0.3 select_reduce_fusion
  134.7 0.4 fusion.32
  135.3 0.2 fusion.30
  135.6 1.0 convolution_convert_fusion.1
  136.6 42.1 %all-to-all-done.3 = bf16[64,8,1792]{2,1,0:T(8,128)(2,1)S(1)} async-done(((bf16[64,8,1792]{2,1,0:T(8,128)(2,1)}), bf16[64,8,1792]{2,1,0:T(8,128)(2,1)S(1)}, u32[]{:S(2)}, u32[]{:S(2)}) %all-to-all-start.3) | async-done | bytes 1835040 | tf_op jit(solution)/shard_map/all_to_all | solution.py:73
  178.7 0.9 gather_fusion
  179.6 1.3 multiply_reduce_fusion
  (32 shorter events, 1.2 us)
Async XLA Ops:
  0.6 134.1 %copy-start = (bf16[4,256,512]{2,1,0:T(8,128)(2,1)S(1)}, bf16[4,256,512]{2,1,0:T(8,128)(2,1)}, u32[]{:S(2)}) copy-start(bf16[4,256,512]{2,1,0:T(8,128)(2,1)} %param.19) | copy-start | bytes 3145732
  5.0 66.7 %all-to-all-start = ((bf16[64,8,1792]{2,1,0:T(8,128)(2,1)}), bf16[64,8,1792]{2,1,0:T(8,128)(2,1)S(1)}, u32[]{:S(2)}, u32[]{:S(2)}) async-start(bf16[64,8,1792]{2,1,0:T(8,128)(2,1)} %fusion.5), calls=%async_computation | async-start | bytes 3670016 | tf_op jit(solution)/shard_map/all_to_all | solution.py:61
  82.5 3.2 %copy-start.7 = (bf16[1,3584,512]{2,1,0:T(8,128)(2,1)S(1)}, bf16[1,3584,512]{2,1,0:T(8,128)(2,1)}, u32[]{:S(2)}) copy-start(bf16[1,3584,512]{2,1,0:T(8,128)(2,1)} %param.14) | copy-start | bytes 11010052
  83.1 5.7 %copy-start.1 = (bf16[64,8,2,1792]{3,1,2,0:T(8,128)(2,1)}, bf16[64,8,2,1792]{3,1,2,0:T(8,128)(2,1)S(1)}, u32[]{:S(2)}) copy-start(bf16[64,8,2,1792]{3,1,2,0:T(8,128)(2,1)S(1)} %copy.32) | copy-start | bytes 11010052
  122.7 9.6 %copy-start.2 = (bf16[1792,64]{0,1:T(8,128)(2,1)S(1)}, bf16[1792,64]{0,1:T(8,128)(2,1)}, u32[]{:S(2)}) copy-start(bf16[1792,64]{0,1:T(8,128)(2,1)} %param.13) | copy-start | bytes 688132
  122.7 9.6 %copy-start.3 = (bf16[16,1792]{1,0:T(8,128)(2,1)S(1)}, bf16[16,1792]{1,0:T(8,128)(2,1)}, u32[]{:S(2)}) copy-start(bf16[16,1792]{1,0:T(8,128)(2,1)} %param.11) | copy-start | bytes 172036
  122.7 12.0 %copy-start.8 = (s32[4]{0:T(128)S(1)}, s32[4]{0:T(128)}, u32[]{:S(2)}) copy-start(s32[4]{0:T(128)} %param.21) | copy-start | bytes 52
  122.7 12.1 %copy-start.4 = (bf16[4,32,512]{2,1,0:T(8,128)(2,1)S(1)}, bf16[4,32,512]{2,1,0:T(8,128)(2,1)}, u32[]{:S(2)}) copy-start(bf16[4,32,512]{2,1,0:T(8,128)(2,1)} %param.17) | copy-start | bytes 393220
  122.7 12.5 %copy-start.5 = (bf16[4,64,256]{2,1,0:T(8,128)(2,1)S(1)}, bf16[4,64,256]{2,1,0:T(8,128)(2,1)}, u32[]{:S(2)}) copy-start(bf16[4,64,256]{2,1,0:T(8,128)(2,1)} %param.20) | copy-start | bytes 393220
  122.7 12.5 %copy-start.6 = (bf16[4,32,64]{2,1,0:T(8,128)(2,1)S(1)}, bf16[4,32,64]{2,1,0:T(8,128)(2,1)}, u32[]{:S(2)}) copy-start(bf16[4,32,64]{2,1,0:T(8,128)(2,1)} %param.18) | copy-start | bytes 49156
  122.7 56.0 %all-to-all-start.3 = ((bf16[64,8,1792]{2,1,0:T(8,128)(2,1)}), bf16[64,8,1792]{2,1,0:T(8,128)(2,1)S(1)}, u32[]{:S(2)}, u32[]{:S(2)}) async-start(bf16[64,8,1792]{2,1,0:T(8,128)(2,1)} %bitcast.59), calls=%async_computation.3 | async-start | bytes 3670016 | tf_op jit(solution)/shard_map/all_to_all | solution.py:73
